TPU v7x, 32 devices: a whole 2x2x4 slice. The times are simulated.
32 devices in a mesh: fsdp: 8 (over y, x, core), dp: 4 (over z).
Axes of the slice: x: 2, y: 2, z: 4, core: 2. Of those that a mesh axis runs over, the one named last changes fastest.
Arguments:
- tokens: bfloat16 [4096, 1536], P(('fsdp', 'dp')), may hold values from -6 to 6
- lengths: int32 [32, 4], P('fsdp'), may hold values from 1 to 64, 128 in all within a row
- cotangent: bfloat16 [4096, 1536], P(('fsdp', 'dp')), may hold values from -6 to 6
- attn_gain: bfloat16 [1, 1536], P(None, 'fsdp'), may hold values from 0.5 to 1.5
- w_query: bfloat16 [1, 1536, 1536], P(None, 'fsdp', 'dp'), may hold values from -0.15625 to 0.15625
- w_key: bfloat16 [1, 1536, 768], P(None, 'fsdp', 'dp'), may hold values from -0.15625 to 0.15625
- w_value: bfloat16 [1, 1536, 768], P(None, 'fsdp', 'dp'), may hold values from -0.15625 to 0.15625
- w_out: bfloat16 [1, 1536, 1536], P(None, 'dp', 'fsdp'), may hold values from -0.875 to 0.875
- mlp_gain: bfloat16 [1, 1536], P(None, 'fsdp'), may hold values from 0.5 to 1.5
- w_gate: bfloat16 [1, 1536, 4096], P(None, 'fsdp', 'dp'), may hold values from -0.15625 to 0.15625
- w_up: bfloat16 [1, 1536, 4096], P(None, 'fsdp', 'dp'), may hold values from -0.15625 to 0.15625
- w_down: bfloat16 [1, 4096, 1536], P(None, 'dp', 'fsdp'), may hold values from -0.09375 to 0.09375
Outputs:
- output: bfloat16 [4096, 1536], P(('fsdp', 'dp'))
- grad_tokens: float32 [4096, 1536], P(('fsdp', 'dp'))
- grad_attn_gain: float32 [1, 1536], P(None, 'fsdp')
- grad_w_query: float32 [1, 1536, 1536], P(None, 'fsdp', 'dp')
- grad_w_key: float32 [1, 1536, 768], P(None, 'fsdp', 'dp')
- grad_w_value: float32 [1, 1536, 768], P(None, 'fsdp', 'dp')
- grad_w_out: float32 [1, 1536, 1536], P(None, 'dp', 'fsdp')
- grad_mlp_gain: float32 [1, 1536], P(None, 'fsdp')
- grad_w_gate: float32 [1, 1536, 4096], P(None, 'fsdp', 'dp')
- grad_w_up: float32 [1, 1536, 4096], P(None, 'fsdp', 'dp')
- grad_w_down: float32 [1, 4096, 1536], P(None, 'dp', 'fsdp')
Inputs may be any that keep to these rules, and one draw needn't show every extreme that they name: `lengths`: each row sums to 128 and its largest entry is 64.
All inputs are finite; a program needn't handle non-finite values.
Results may differ from a plain program's by a relative error of at most 0.019.
Values may be sent and summed in bfloat16 or wider, within the bound.
A program may use at most 320 MiB of HBM per device.

v0:
```python
from functools import partial
import jax
import jax.numpy as jnp
from jax import lax
from jax.sharding import PartitionSpec as P

HD = 96
LAYERS = 1
EPSILON = 1e-05
ROPE_BASE = 100000.0
NEG_FILL = -1e30


def layout(seq_lengths, rows_here):
    seg_ends = jnp.cumsum(seq_lengths)
    seg_starts = seg_ends - seq_lengths
    positions = jnp.arange(rows_here, dtype=jnp.int32)
    segment = jnp.sum((positions[:, None] >= seg_ends[None, :]).astype(jnp.int32), axis=1)
    member = segment[:, None] == jnp.arange(seq_lengths.shape[0], dtype=jnp.int32)[None, :]
    offset = jnp.sum(jnp.where(member, seg_starts[None, :], 0), axis=1)
    where_in = positions - offset
    allowed = (segment[:, None] == segment[None, :]) & (positions[None, :] <= positions[:, None])
    half_dim = HD // 2
    frequency = ROPE_BASE ** (-jnp.arange(half_dim, dtype=jnp.float32) / half_dim)
    angles = where_in.astype(jnp.float32)[:, None] * frequency[None, :]
    return (allowed, jnp.cos(angles), jnp.sin(angles))


def rotate(values, cosine, sine_tab, sign_flip):
    half_dim = values.shape[-1] // 2
    front_half = values[..., :half_dim]
    back_half = values[..., half_dim:]
    cos_part = cosine[:, None, :]
    sin_part = sign_flip * sine_tab[:, None, :]
    return jnp.concatenate(
        [
            front_half * cos_part - back_half * sin_part,
            back_half * cos_part + front_half * sin_part,
        ],
        axis=-1,
    )


def rms_scale(stream):
    return lax.rsqrt(jnp.mean(stream * stream, axis=-1, keepdims=True) + EPSILON)


def matmul(left, right):
    return jnp.dot(left, right, preferred_element_type=jnp.float32)


def inner_rows(left, right):
    return lax.dot_general(
        left, right, (((0,), (0,)), ((), ())), preferred_element_type=jnp.float32
    )


def times_transposed(left, right):
    return lax.dot_general(
        left, right, (((1,), (1,)), ((), ())), preferred_element_type=jnp.float32
    )


def attend(queries, keys_rot, values_in, allowed):
    rows_here = queries.shape[0]
    kv_heads = keys_rot.shape[1]
    grouped = queries.reshape(rows_here, kv_heads, queries.shape[1] // kv_heads, HD)
    scores = jnp.einsum(
        "qkgd,skd->kgqs", grouped, keys_rot, preferred_element_type=jnp.float32
    ) * HD ** (-0.5)
    scores = jnp.where(allowed[None, None], scores, NEG_FILL)
    row_top = jnp.max(scores, axis=-1, keepdims=True)
    log_total = row_top + jnp.log(jnp.sum(jnp.exp(scores - row_top), axis=-1, keepdims=True))
    attn_probs = jnp.where(allowed[None, None], jnp.exp(scores - log_total), 0.0)
    probs_low = attn_probs.astype(jnp.bfloat16)
    attn_mixed = jnp.einsum(
        "kgqs,skd->qkgd", probs_low, values_in, preferred_element_type=jnp.float32
    )
    return (attn_probs, attn_mixed.reshape(rows_here, queries.shape[1] * HD).astype(jnp.bfloat16))


def attend_back(queries, keys_rot, values_in, attn_probs, attn_mixed, grad_mixed):
    rows_here = queries.shape[0]
    kv_heads = keys_rot.shape[1]
    groups = queries.shape[1] // kv_heads
    grouped = queries.reshape(rows_here, kv_heads, groups, HD)
    grad_grouped = grad_mixed.reshape(rows_here, kv_heads, groups, HD)
    mixed_grouped = attn_mixed.reshape(rows_here, kv_heads, groups, HD)
    delta = jnp.sum(grad_grouped.astype(jnp.float32) * mixed_grouped.astype(jnp.float32), axis=-1)
    delta = jnp.transpose(delta, (1, 2, 0))[..., None]
    grad_probs = jnp.einsum(
        "qkgd,skd->kgqs", grad_grouped, values_in, preferred_element_type=jnp.float32
    )
    grad_score = (attn_probs * (grad_probs - delta) * HD ** (-0.5)).astype(jnp.bfloat16)
    probs_low = attn_probs.astype(jnp.bfloat16)
    grad_q = jnp.einsum(
        "kgqs,skd->qkgd", grad_score, keys_rot, preferred_element_type=jnp.float32
    ).reshape(rows_here, queries.shape[1], HD)
    grad_k = jnp.einsum("kgqs,qkgd->skd", grad_score, grouped, preferred_element_type=jnp.float32)
    grad_v = jnp.einsum(
        "kgqs,qkgd->skd", probs_low, grad_grouped, preferred_element_type=jnp.float32
    )
    return (grad_q, grad_k, grad_v)


def by_blocks(array_in, count):
    return array_in.reshape((count, array_in.shape[0] // count) + array_in.shape[1:])


def from_blocks(array_in):
    return array_in.reshape((array_in.shape[0] * array_in.shape[1],) + array_in.shape[2:])


def attend_blocks(queries, keys_rot, values_in, allowed):
    count = allowed.shape[0]
    attn_probs, attn_mixed = jax.vmap(attend)(
        by_blocks(queries, count), by_blocks(keys_rot, count), by_blocks(values_in, count), allowed
    )
    return (attn_probs, from_blocks(attn_mixed))


def attend_back_blocks(queries, keys_rot, values_in, attn_probs, attn_mixed, grad_mixed):
    count = attn_probs.shape[0]
    grad_q, grad_k, grad_v = jax.vmap(attend_back)(
        by_blocks(queries, count),
        by_blocks(keys_rot, count),
        by_blocks(values_in, count),
        attn_probs,
        by_blocks(attn_mixed, count),
        by_blocks(grad_mixed, count),
    )
    return (from_blocks(grad_q), from_blocks(grad_k), from_blocks(grad_v))


def layer_forward(stream, weights, allowed, cosine, sine_tab, spread, settle):
    attn_gain, w_query, w_key, w_value, w_out, mlp_gain, w_gate, w_up, w_down = weights
    scale_one = rms_scale(stream)
    normed_one = stream * scale_one
    attn_in = spread((normed_one * attn_gain.astype(jnp.float32)).astype(jnp.bfloat16))
    rows_here = attn_in.shape[0]
    queries = rotate(
        matmul(attn_in, w_query).reshape(rows_here, w_query.shape[1] // HD, HD),
        cosine,
        sine_tab,
        1.0,
    ).astype(jnp.bfloat16)
    keys_rot = rotate(
        matmul(attn_in, w_key).reshape(rows_here, w_key.shape[1] // HD, HD), cosine, sine_tab, 1.0
    ).astype(jnp.bfloat16)
    values_in = (
        matmul(attn_in, w_value).reshape(rows_here, w_value.shape[1] // HD, HD).astype(jnp.bfloat16)
    )
    attn_probs, attn_mixed = attend_blocks(queries, keys_rot, values_in, allowed)
    middle = stream + settle(matmul(attn_mixed, w_out))
    scale_two = rms_scale(middle)
    normed_two = middle * scale_two
    mlp_in = spread((normed_two * mlp_gain.astype(jnp.float32)).astype(jnp.bfloat16))
    gate_act = matmul(mlp_in, w_gate)
    up_act = matmul(mlp_in, w_up)
    hidden = (jax.nn.silu(gate_act) * up_act).astype(jnp.bfloat16)
    result = middle + settle(matmul(hidden, w_down))
    kept_state = (
        scale_one,
        normed_one,
        attn_in,
        queries,
        keys_rot,
        values_in,
        attn_probs,
        attn_mixed,
        scale_two,
        normed_two,
        mlp_in,
        gate_act,
        up_act,
        hidden,
    )
    return (result, kept_state)


def layer_backward(stream, weights, allowed, cosine, sine_tab, grad_stream, spread, settle):
    attn_gain, w_query, w_key, w_value, w_out, mlp_gain, w_gate, w_up, w_down = weights
    _, kept_state = layer_forward(stream, weights, allowed, cosine, sine_tab, spread, settle)
    (
        scale_one,
        normed_one,
        attn_in,
        queries,
        keys_rot,
        values_in,
        attn_probs,
        attn_mixed,
        scale_two,
        normed_two,
        mlp_in,
        gate_act,
        up_act,
        hidden,
    ) = kept_state
    rows_here = attn_in.shape[0]
    grad_low = spread(grad_stream.astype(jnp.bfloat16))
    grad_down = inner_rows(hidden, grad_low)
    grad_hidden = times_transposed(grad_low, w_down)
    sigmoid_gate = jax.nn.sigmoid(gate_act)
    grad_up_act = (grad_hidden * gate_act * sigmoid_gate).astype(jnp.bfloat16)
    grad_gate_act = (
        grad_hidden * up_act * sigmoid_gate * (1.0 + gate_act * (1.0 - sigmoid_gate))
    ).astype(jnp.bfloat16)
    grad_gate = inner_rows(mlp_in, grad_gate_act)
    grad_up = inner_rows(mlp_in, grad_up_act)
    grad_mlp_in = settle(
        times_transposed(grad_gate_act, w_gate) + times_transposed(grad_up_act, w_up)
    )
    grad_mlp_gain = jnp.sum(grad_mlp_in * normed_two, axis=0)
    grad_normed = grad_mlp_in * mlp_gain.astype(jnp.float32)
    grad_middle = grad_stream + scale_two * (
        grad_normed - normed_two * jnp.mean(grad_normed * normed_two, axis=-1, keepdims=True)
    )
    grad_middle_low = spread(grad_middle.astype(jnp.bfloat16))
    grad_out = inner_rows(attn_mixed, grad_middle_low)
    grad_mixed = times_transposed(grad_middle_low, w_out).astype(jnp.bfloat16)
    grad_q, grad_k, grad_v = attend_back_blocks(
        queries, keys_rot, values_in, attn_probs, attn_mixed, grad_mixed
    )
    grad_q = (
        rotate(grad_q, cosine, sine_tab, -1.0)
        .reshape(rows_here, w_query.shape[1])
        .astype(jnp.bfloat16)
    )
    grad_k = (
        rotate(grad_k, cosine, sine_tab, -1.0)
        .reshape(rows_here, w_key.shape[1])
        .astype(jnp.bfloat16)
    )
    grad_v = grad_v.reshape(rows_here, w_value.shape[1]).astype(jnp.bfloat16)
    grad_query = inner_rows(attn_in, grad_q)
    grad_key = inner_rows(attn_in, grad_k)
    grad_value = inner_rows(attn_in, grad_v)
    grad_attn_in = settle(
        times_transposed(grad_q, w_query)
        + times_transposed(grad_k, w_key)
        + times_transposed(grad_v, w_value)
    )
    grad_attn_gain = jnp.sum(grad_attn_in * normed_one, axis=0)
    grad_normed_one = grad_attn_in * attn_gain.astype(jnp.float32)
    grad_input = grad_middle + scale_one * (
        grad_normed_one
        - normed_one * jnp.mean(grad_normed_one * normed_one, axis=-1, keepdims=True)
    )
    return (
        grad_input,
        (
            grad_attn_gain,
            grad_query,
            grad_key,
            grad_value,
            grad_out,
            grad_mlp_gain,
            grad_gate,
            grad_up,
            grad_down,
        ),
    )


def fetch_fsdp(shards, layer_idx):
    return (
        lax.all_gather(shards[1][layer_idx], "fsdp", axis=0, tiled=True),
        lax.all_gather(shards[2][layer_idx], "fsdp", axis=0, tiled=True),
        lax.all_gather(shards[3][layer_idx], "fsdp", axis=0, tiled=True),
        lax.all_gather(shards[4][layer_idx], "fsdp", axis=1, tiled=True),
        lax.all_gather(shards[6][layer_idx], "fsdp", axis=0, tiled=True),
        lax.all_gather(shards[7][layer_idx], "fsdp", axis=0, tiled=True),
        lax.all_gather(shards[8][layer_idx], "fsdp", axis=1, tiled=True),
        lax.all_gather(shards[0][layer_idx], "fsdp", axis=0, tiled=True),
        lax.all_gather(shards[5][layer_idx], "fsdp", axis=0, tiled=True),
    )


def fetch_fsdp_back(shards, layer_idx):
    return (
        lax.all_gather(shards[1][layer_idx], "fsdp", axis=0, tiled=True),
        lax.all_gather(shards[2][layer_idx], "fsdp", axis=0, tiled=True),
        lax.all_gather(shards[3][layer_idx], "fsdp", axis=0, tiled=True),
        lax.all_gather(shards[4][layer_idx], "fsdp", axis=1, tiled=True),
        lax.all_gather(shards[6][layer_idx], "fsdp", axis=0, tiled=True),
        lax.all_gather(shards[7][layer_idx], "fsdp", axis=0, tiled=True),
        lax.all_gather(shards[8][layer_idx], "fsdp", axis=1, tiled=True),
        lax.all_gather(shards[0][layer_idx], "fsdp", axis=0, tiled=True),
        lax.all_gather(shards[5][layer_idx], "fsdp", axis=0, tiled=True),
    )


def arrange(matrices, pieces):
    return (
        pieces[7],
        matrices[0],
        matrices[1],
        matrices[2],
        matrices[3],
        pieces[8],
        matrices[4],
        matrices[5],
        matrices[6],
    )


def body(
    tokens,
    lengths,
    cotangent,
    attn_gain,
    w_query,
    w_key,
    w_value,
    w_out,
    mlp_gain,
    w_gate,
    w_up,
    w_down,
):
    shards = (attn_gain, w_query, w_key, w_value, w_out, mlp_gain, w_gate, w_up, w_down)

    def spread(rows_in):
        return lax.all_gather(rows_in, "dp", axis=0, tiled=True)

    def settle(terms_in):
        return lax.psum_scatter(
            terms_in.astype(jnp.bfloat16), "dp", scatter_dimension=0, tiled=True
        ).astype(jnp.float32)

    allowed, cosine, sine_tab = jax.vmap(partial(layout, rows_here=tokens.shape[0]))(lengths)
    cosine = from_blocks(cosine)
    sine_tab = from_blocks(sine_tab)
    stream = tokens.astype(jnp.float32)
    weights_kept = []
    layer_idx = 0
    pieces = fetch_fsdp(shards, layer_idx)
    weights = arrange(pieces[:7], pieces)
    weights_kept.append(weights)
    inputs_kept = [stream]
    stream, _ = layer_forward(stream, weights, allowed, cosine, sine_tab, spread, settle)
    output = stream.astype(jnp.bfloat16)
    grad_stream = cotangent.astype(jnp.float32)
    grads_by_layer = [None] * LAYERS
    for layer_idx in reversed(range(LAYERS)):
        weights = weights_kept[layer_idx]
        grad_stream, terms = layer_backward(
            inputs_kept[layer_idx], weights, allowed, cosine, sine_tab, grad_stream, spread, settle
        )
        gains = lax.psum((terms[0], terms[5]), "dp")
        owned = (
            lax.psum_scatter(
                terms[1].astype(jnp.bfloat16), "fsdp", scatter_dimension=0, tiled=True
            ).astype(jnp.float32),
            lax.psum_scatter(
                terms[2].astype(jnp.bfloat16), "fsdp", scatter_dimension=0, tiled=True
            ).astype(jnp.float32),
            lax.psum_scatter(
                terms[3].astype(jnp.bfloat16), "fsdp", scatter_dimension=0, tiled=True
            ).astype(jnp.float32),
            lax.psum_scatter(
                terms[4].astype(jnp.bfloat16), "fsdp", scatter_dimension=1, tiled=True
            ).astype(jnp.float32),
            lax.psum_scatter(
                terms[6].astype(jnp.bfloat16), "fsdp", scatter_dimension=0, tiled=True
            ).astype(jnp.float32),
            lax.psum_scatter(
                terms[7].astype(jnp.bfloat16), "fsdp", scatter_dimension=0, tiled=True
            ).astype(jnp.float32),
            lax.psum_scatter(
                terms[8].astype(jnp.bfloat16), "fsdp", scatter_dimension=1, tiled=True
            ).astype(jnp.float32),
            lax.psum_scatter(
                gains[0].astype(jnp.bfloat16), "fsdp", scatter_dimension=0, tiled=True
            ).astype(jnp.float32),
            lax.psum_scatter(
                gains[1].astype(jnp.bfloat16), "fsdp", scatter_dimension=0, tiled=True
            ).astype(jnp.float32),
        )
        grads_by_layer[layer_idx] = arrange(owned, owned)
    stacked = tuple((jnp.stack([grads_by_layer[0][slot_idx]]) for slot_idx in range(9)))
    return (output, grad_stream) + stacked


def solution(mesh):
    placed = (
        P(("fsdp", "dp"), None),
        P("fsdp", None),
        P(("fsdp", "dp"), None),
        P(None, "fsdp"),
        P(None, "fsdp", "dp"),
        P(None, "fsdp", "dp"),
        P(None, "fsdp", "dp"),
        P(None, "dp", "fsdp"),
        P(None, "fsdp"),
        P(None, "fsdp", "dp"),
        P(None, "fsdp", "dp"),
        P(None, "dp", "fsdp"),
    )
    return jax.shard_map(
        body,
        mesh=mesh,
        in_specs=placed,
        out_specs=(
            P(("fsdp", "dp"), None),
            P(("fsdp", "dp"), None),
            P(None, "fsdp"),
            P(None, "fsdp", "dp"),
            P(None, "fsdp", "dp"),
            P(None, "fsdp", "dp"),
            P(None, "dp", "fsdp"),
            P(None, "fsdp"),
            P(None, "fsdp", "dp"),
            P(None, "fsdp", "dp"),
            P(None, "dp", "fsdp"),
        ),
        check_vma=False,
    )
```

profile of v0, /device:TPU:0, one launch (start us, length us, event | category | flops | bytes accessed | tf_op | source)
XLA Modules:
  0.0 808.7 jit_solution(16388538002550053874)
XLA Ops:
  12.3 16.0 %all-reduce.6 = (bf16[1536]{0:T(1024)(128)(2,1)S(1)}, bf16[1536]{0:T(1024)(128)(2,1)}) all-reduce(bf16[1536]{0:T(1024)(128)(2,1)S(1)} %dynamic-update-slice, bf16[1536]{0:T(1024)(128)(2,1)S(1)} %dynamic-update-slice.1), channel_id=2, replica_groups=mesh['fsdp'=8,'dp'=4] {'fsdp'}, use_global_device_ids=true, to_apply=%add | all-reduce | flops 3072 | bytes 12288
  32.4 9.4 %all-gather.2 = bf16[1,1536,192]{2,1,0:T(8,128)(2,1)S(1)} all-gather(bf16[1,192,192]{2,1,0:T(8,128)(2,1)S(1)} %copy-done.29), channel_id=4, replica_groups=mesh['fsdp'=8,'dp'=4] {'fsdp'}, dimensions={1}, use_global_device_ids=true | all-gather | bytes 663552 | tf_op jit(solution)/shard_map/all_gather | solution.py:269
  41.8 10.3 %all-gather.1 = bf16[1,1536,192]{2,1,0:T(8,128)(2,1)S(1)} all-gather(bf16[1,192,192]{2,1,0:T(8,128)(2,1)S(1)} %copy-done.30), channel_id=3, replica_groups=mesh['fsdp'=8,'dp'=4] {'fsdp'}, dimensions={1}, use_global_device_ids=true | all-gather | bytes 663552 | tf_op jit(solution)/shard_map/all_gather | solution.py:270
  53.3 13.6 %all-gather.19.cloned.1.call-done = bf16[512,1536]{1,0:T(8,128)(2,1)} async-done(((bf16[128,1536]{1,0:T(8,128)(2,1)}), bf16[512,1536]{1,0:T(8,128)(2,1)}) %all-gather.19.cloned.1.call-update) | async-done | bytes 1572880 | tf_op jit(solution)/shard_map/all_gather | solution.py:325
  71.4 20.2 %all-gather.27.cloned.1.call-done = bf16[1,1536,384]{2,1,0:T(8,128)(2,1)} async-done(((bf16[1,192,384]{2,1,0:T(8,128)(2,1)}), bf16[1,1536,384]{2,1,0:T(8,128)(2,1)}) %all-gather.27.cloned.1.call-update) | async-done | bytes 1179664 | tf_op jit(solution)/shard_map/all_gather | solution.py:268
  96.5 20.8 %all-gather.29.cloned.1.call-done = bf16[1,384,1536]{1,2,0:T(8,128)(2,1)} async-done(((bf16[1,384,192]{1,2,0:T(8,128)(2,1)}), bf16[1,384,1536]{1,2,0:T(8,128)(2,1)}) %all-gather.29.cloned.1.call-update) | async-done | bytes 1179664 | tf_op jit(solution)/shard_map/all_gather | solution.py:271
  121.5 34.9 %reduce-scatter.12.cloned.1.call-done = bf16[128,1536]{1,0:T(8,128)(2,1)} async-done(((bf16[512,1536]{1,0:T(8,128)(2,1)}), bf16[128,1536]{1,0:T(8,128)(2,1)}) %reduce-scatter.12.cloned.1.call-update) | async-done | bytes 393232 | tf_op jit(solution)/shard_map/reduce_scatter | solution.py:328
  162.1 27.2 %all-gather.33.cloned.1.call-done = bf16[1,1536,1024]{2,1,0:T(8,128)(2,1)} async-done(((bf16[1,192,1024]{2,1,0:T(8,128)(2,1)}), bf16[1,1536,1024]{2,1,0:T(8,128)(2,1)}) %all-gather.33.cloned.1.call-update) | async-done | bytes 3145744 | tf_op jit(solution)/shard_map/all_gather | solution.py:273
  189.3 39.1 %all-gather.21.cloned.1.call-done = bf16[512,1536]{1,0:T(8,128)(2,1)} async-done(((bf16[128,1536]{1,0:T(8,128)(2,1)}), bf16[512,1536]{1,0:T(8,128)(2,1)}) %all-gather.21.cloned.1.call-update) | async-done | bytes 1572880 | tf_op jit(solution)/shard_map/all_gather | solution.py:325
  228.3 5.6 fusion.5
  233.9 27.4 %all-gather.31.cloned.1.call-done = bf16[1,1536,1024]{2,1,0:T(8,128)(2,1)} async-done(((bf16[1,192,1024]{2,1,0:T(8,128)(2,1)}), bf16[1,1536,1024]{2,1,0:T(8,128)(2,1)}) %all-gather.31.cloned.1.call-update) | async-done | bytes 3145744 | tf_op jit(solution)/shard_map/all_gather | solution.py:272
  261.3 5.5 fusion.9
  266.8 33.1 %all-gather.23.cloned.1.call-done = bf16[512,1536]{1,0:T(8,128)(2,1)} async-done(((bf16[128,1536]{1,0:T(8,128)(2,1)}), bf16[512,1536]{1,0:T(8,128)(2,1)}) %all-gather.23.cloned.1.call-update) | async-done | bytes 1572880 | tf_op jit(solution)/shard_map/all_gather | solution.py:325
  299.9 33.0 %all-gather.35.cloned.1.call-done = bf16[1,1024,1536]{1,2,0:T(8,128)(2,1)} async-done(((bf16[1,1024,192]{1,2,0:T(8,128)(2,1)}), bf16[1,1024,1536]{1,2,0:T(8,128)(2,1)}) %all-gather.35.cloned.1.call-update) | async-done | bytes 3145744 | tf_op jit(solution)/shard_map/all_gather | solution.py:274
  332.9 7.2 multiply_convert_fusion
  345.8 35.5 %reduce-scatter.16.cloned.1.call-done = bf16[128,1536]{1,0:T(8,128)(2,1)} async-done(((bf16[512,1536]{1,0:T(8,128)(2,1)}), bf16[128,1536]{1,0:T(8,128)(2,1)}) %reduce-scatter.16.cloned.1.call-update) | async-done | bytes 393232 | tf_op jit(solution)/shard_map/reduce_scatter | solution.py:328
  385.6 5.3 convolution_convert_fusion
  391.0 5.4 convolution_convert_fusion.1
  396.7 5.2 convolution_convert_fusion.2
  402.0 19.7 %all-gather.25.cloned.1.call-done = bf16[512,1536]{1,0:T(8,128)(2,1)} async-done(((bf16[128,1536]{1,0:T(8,128)(2,1)}), bf16[512,1536]{1,0:T(8,128)(2,1)}) %all-gather.25.cloned.1.call-update) | async-done | bytes 1572880 | tf_op jit(solution)/shard_map/all_gather | solution.py:325
  452.7 4.9 fusion.11
  458.3 11.5 %reduce-scatter.32.cloned.1.call-done = bf16[1024,192]{0,1:T(8,128)(2,1)} async-done(((bf16[1024,1536]{0,1:T(8,128)(2,1)}), bf16[1024,192]{0,1:T(8,128)(2,1)}) %reduce-scatter.32.cloned.1.call-update) | async-done | bytes 393232 | tf_op jit(solution)/shard_map/reduce_scatter | solution.py:371
  471.8 47.6 %reduce-scatter.30.cloned.1.call-done = bf16[192,1024]{1,0:T(8,128)(2,1)} async-done(((bf16[1536,1024]{1,0:T(8,128)(2,1)}), bf16[192,1024]{1,0:T(8,128)(2,1)}) %reduce-scatter.30.cloned.1.call-update) | async-done | bytes 393232 | tf_op jit(solution)/shard_map/reduce_scatter | solution.py:368
  521.3 47.3 %reduce-scatter.28.cloned.1.call-done = bf16[192,1024]{1,0:T(8,128)(2,1)} async-done(((bf16[1536,1024]{1,0:T(8,128)(2,1)}), bf16[192,1024]{1,0:T(8,128)(2,1)}) %reduce-scatter.28.cloned.1.call-update) | async-done | bytes 393232 | tf_op jit(solution)/shard_map/reduce_scatter | solution.py:365
  570.6 36.0 %reduce-scatter.24.cloned.1.call-done = bf16[192,192]{1,0:T(8,128)(2,1)} async-done(((bf16[1536,192]{1,0:T(8,128)(2,1)}), bf16[192,192]{1,0:T(8,128)(2,1)}) %reduce-scatter.24.cloned.1.call-update) | async-done | bytes 73744 | tf_op jit(solution)/shard_map/reduce_scatter | solution.py:359
  608.2 37.0 %reduce-scatter.22.cloned.1.call-done = bf16[192,192]{1,0:T(8,128)(2,1)} async-done(((bf16[1536,192]{1,0:T(8,128)(2,1)}), bf16[192,192]{1,0:T(8,128)(2,1)}) %reduce-scatter.22.cloned.1.call-update) | async-done | bytes 73744 | tf_op jit(solution)/shard_map/reduce_scatter | solution.py:356
  646.7 38.2 %reduce-scatter.26.cloned.1.call-done = bf16[384,192]{0,1:T(8,128)(2,1)} async-done(((bf16[384,1536]{0,1:T(8,128)(2,1)}), bf16[384,192]{0,1:T(8,128)(2,1)}) %reduce-scatter.26.cloned.1.call-update) | async-done | bytes 147472 | tf_op jit(solution)/shard_map/reduce_scatter | solution.py:362
  686.6 38.2 %reduce-scatter.20.cloned.1.call-done = bf16[192,384]{1,0:T(8,128)(2,1)} async-done(((bf16[1536,384]{1,0:T(8,128)(2,1)}), bf16[192,384]{1,0:T(8,128)(2,1)}) %reduce-scatter.20.cloned.1.call-update) | async-done | bytes 147472 | tf_op jit(solution)/shard_map/reduce_scatter | solution.py:353
  726.4 36.1 %reduce-scatter.18.cloned.1.call-done = bf16[128,1536]{1,0:T(8,128)(2,1)} async-done(((bf16[512,1536]{1,0:T(8,128)(2,1)}), bf16[128,1536]{1,0:T(8,128)(2,1)}) %reduce-scatter.18.cloned.1.call-update) | async-done | bytes 393232 | tf_op jit(solution)/shard_map/reduce_scatter | solution.py:328
  763.8 17.3 %all-reduce.4 = (bf16[1536]{0:T(1024)(128)(2,1)S(1)}, bf16[1536]{0:T(1024)(128)(2,1)S(1)}) all-reduce(f32[1536]{0:T(1024)S(1)} %get-tuple-element.13, f32[1536]{0:T(1024)S(1)} %copy-done.31), channel_id=1, replica_groups=mesh['fsdp'=8,'dp'=4] {'dp'}, use_global_device_ids=true, to_apply=%region_15.16 | all-reduce | flops 3072 | bytes 18432 | tf_op jit(solution)/shard_map/psum | solution.py:351
  781.1 12.5 %all-reduce.5 = (bf16[1536]{0:T(1024)(128)(2,1)S(1)}, bf16[1536]{0:T(1024)(128)(2,1)S(1)}) all-reduce(bf16[1536]{0:T(1024)(128)(2,1)S(1)} %get-tuple-element.15, bf16[1536]{0:T(1024)(128)(2,1)S(1)} %get-tuple-element.16), channel_id=15, replica_groups=mesh['fsdp'=8,'dp'=4] {'fsdp'}, use_global_device_ids=true, to_apply=%region_16.17.clone | all-reduce | flops 3072 | bytes 12288
  794.9 4.2 reduce-scatter.14.cloned.1.call-done
  (211 shorter events, 87.4 us)
Async XLA Ops:
  7.2 59.6 %all-gather.19.cloned.1.call-start = ((), (), s32[]{:S(2)}) async-start(), calls=%async_computation.11 | async-start | bytes 1966080 | tf_op jit(solution)/shard_map/all_gather | solution.py:325
  30.3 61.2 %all-gather.27.cloned.1.call-start = ((), (), s32[]{:S(2)}) async-start(), calls=%async_computation.26 | async-start | bytes 1327104 | tf_op jit(solution)/shard_map/all_gather | solution.py:268
  31.0 86.3 %all-gather.29.cloned.1.call-start = ((), (), s32[]{:S(2)}) async-start(), calls=%async_computation.27 | async-start | bytes 1327104 | tf_op jit(solution)/shard_map/all_gather | solution.py:271
  31.8 124.7 %reduce-scatter.12.cloned.1.call-start = ((), (), s32[]{:S(2)}) async-start(), calls=%async_computation.12 | async-start | bytes 1966080 | tf_op jit(solution)/shard_map/reduce_scatter | solution.py:328
  32.4 63.0 %copy-start.18 = (pred[4,128,128]{1,2,0:T(8,128)(4,1)}, pred[4,128,128]{1,2,0:T(8,128)(4,1)S(1)}, u32[]{:S(2)}) copy-start(pred[4,128,128]{1,2,0:T(8,128)(4,1)S(1)} %compare_and_fusion) | copy-start | bytes 196612
  41.8 52.1 %copy-start.3 = (bf16[1,1536,192]{2,1,0:T(8,128)(2,1)}, bf16[1,1536,192]{2,1,0:T(8,128)(2,1)S(1)}, u32[]{:S(2)}) copy-start(bf16[1,1536,192]{2,1,0:T(8,128)(2,1)S(1)} %all-gather.2) | copy-start | bytes 1769476
  53.3 41.3 %copy-start.14 = (f32[512,48]{0,1:T(8,128)}, f32[512,48]{0,1:T(8,128)S(1)}, u32[]{:S(2)}) copy-start(f32[512,48]{0,1:T(8,128)S(1)} %get-tuple-element.36) | copy-start | bytes 294916
  120.9 35.6 %copy-start = (bf16[128,1536]{1,0:T(8,128)(2,1)S(1)}, bf16[128,1536]{1,0:T(8,128)(2,1)}, u32[]{:S(2)}) copy-start(bf16[128,1536]{1,0:T(8,128)(2,1)} %param.12) | copy-start | bytes 1179652
  120.9 68.4 %all-gather.33.cloned.1.call-start = ((), (), s32[]{:S(2)}) async-start(), calls=%async_computation.29 | async-start | bytes 3538944 | tf_op jit(solution)/shard_map/all_gather | solution.py:273
  121.5 106.9 %all-gather.21.cloned.1.call-start = ((), (), s32[]{:S(2)}) async-start(), calls=%async_computation.13 | async-start | bytes 1966080 | tf_op jit(solution)/shard_map/all_gather | solution.py:325
  157.7 225.7 %copy-start.32 = (f32[128]{0:T(128)}, f32[128]{0:T(128)S(1)}, u32[]{:S(2)}) copy-start(f32[128]{0:T(128)S(1)} %add_rsqrt_fusion) | copy-start | bytes 1540
  159.6 101.7 %all-gather.31.cloned.1.call-start = ((), (), s32[]{:S(2)}) async-start(), calls=%async_computation.28 | async-start | bytes 3538944 | tf_op jit(solution)/shard_map/all_gather | solution.py:272
  160.4 139.5 %all-gather.23.cloned.1.call-start = ((), (), s32[]{:S(2)}) async-start(), calls=%async_computation.15 | async-start | bytes 1966080 | tf_op jit(solution)/shard_map/all_gather | solution.py:325
  161.1 171.8 %all-gather.35.cloned.1.call-start = ((), (), s32[]{:S(2)}) async-start(), calls=%async_computation.30 | async-start | bytes 3538944 | tf_op jit(solution)/shard_map/all_gather | solution.py:274
  161.9 219.5 %reduce-scatter.16.cloned.1.call-start = ((), (), s32[]{:S(2)}) async-start(), calls=%async_computation.16 | async-start | bytes 1966080 | tf_op jit(solution)/shard_map/reduce_scatter | solution.py:328
  345.8 35.6 %copy-start.2 = (bf16[128,1536]{1,0:T(8,128)(2,1)S(1)}, bf16[128,1536]{1,0:T(8,128)(2,1)}, u32[]{:S(2)}) copy-start(bf16[128,1536]{1,0:T(8,128)(2,1)} %reduce-scatter.12.cloned.1.call-done) | copy-start | bytes 1179652
  345.8 75.8 %all-gather.25.cloned.1.call-start = ((), (), s32[]{:S(2)}) async-start(), calls=%async_computation.17 | async-start | bytes 1966080 | tf_op jit(solution)/shard_map/all_gather | solution.py:325
  385.6 84.2 %reduce-scatter.32.cloned.1.call-start = ((), (), s32[]{:S(2)}) async-start(), calls=%async_computation.25 | async-start | bytes 3538944 | tf_op jit(solution)/shard_map/reduce_scatter | solution.py:371
  390.9 128.4 %reduce-scatter.30.cloned.1.call-start = ((), (), s32[]{:S(2)}) async-start(), calls=%async_computation.24 | async-start | bytes 3538944 | tf_op jit(solution)/shard_map/reduce_scatter | solution.py:368
  396.4 172.2 %reduce-scatter.28.cloned.1.call-start = ((), (), s32[]{:S(2)}) async-start(), calls=%async_computation.23 | async-start | bytes 3538944 | tf_op jit(solution)/shard_map/reduce_scatter | solution.py:365
  401.9 204.7 %reduce-scatter.24.cloned.1.call-start = ((), (), s32[]{:S(2)}) async-start(), calls=%async_computation.21 | async-start | bytes 884736 | tf_op jit(solution)/shard_map/reduce_scatter | solution.py:359
  433.8 211.4 %reduce-scatter.22.cloned.1.call-start = ((), (), s32[]{:S(2)}) async-start(), calls=%async_computation.20 | async-start | bytes 884736 | tf_op jit(solution)/shard_map/reduce_scatter | solution.py:356
  437.0 247.9 %reduce-scatter.26.cloned.1.call-start = ((), (), s32[]{:S(2)}) async-start(), calls=%async_computation.22 | async-start | bytes 1327104 | tf_op jit(solution)/shard_map/reduce_scatter | solution.py:362
  440.7 284.0 %reduce-scatter.20.cloned.1.call-start = ((), (), s32[]{:S(2)}) async-start(), calls=%async_computation.19 | async-start | bytes 1327104 | tf_op jit(solution)/shard_map/reduce_scatter | solution.py:353
  446.1 316.3 %reduce-scatter.18.cloned.1.call-start = ((), (), s32[]{:S(2)}) async-start(), calls=%async_computation.18 | async-start | bytes 1966080 | tf_op jit(solution)/shard_map/reduce_scatter | solution.py:328
  451.5 347.6 %reduce-scatter.14.cloned.1.call-start = ((), (), s32[]{:S(2)}) async-start(), calls=%async_computation.14 | async-start | bytes 1966080 | tf_op jit(solution)/shard_map/reduce_scatter | solution.py:328
  521.3 241.2 %copy-start.36 = (f32[128]{0:T(128)S(1)}, f32[128]{0:T(128)}, u32[]{:S(2)}) copy-start(f32[128]{0:T(128)} %copy-done.35) | copy-start | bytes 1540
  521.3 242.6 %copy-start.31 = (f32[1536]{0:T(1024)S(1)}, f32[1536]{0:T(1024)}, u32[]{:S(2)}) copy-start(f32[1536]{0:T(1024)} %get-tuple-element.11) | copy-start | bytes 18436
  521.3 277.9 %copy-start.7 = (bf16[128,1536]{1,0:T(8,128)(2,1)S(1)}, bf16[128,1536]{1,0:T(8,128)(2,1)}, u32[]{:S(2)}) copy-start(bf16[128,1536]{1,0:T(8,128)(2,1)} %param.14) | copy-start | bytes 1179652
  521.3 277.9 %copy-start.8 = (bf16[128,1536]{1,0:T(8,128)(2,1)S(1)}, bf16[128,1536]{1,0:T(8,128)(2,1)}, u32[]{:S(2)}) copy-start(bf16[128,1536]{1,0:T(8,128)(2,1)} %reduce-scatter.16.cloned.1.call-done) | copy-start | bytes 1179652
  521.3 277.9 %copy-start.33 = (f32[128]{0:T(128)S(1)}, f32[128]{0:T(128)}, u32[]{:S(2)}) copy-start(f32[128]{0:T(128)} %copy-done.32) | copy-start | bytes 1540
  521.3 277.9 %copy-start.39 = (f32[128]{0:T(128)S(1)}, f32[128]{0:T(128)}, u32[]{:S(2)}) copy-start(f32[128]{0:T(128)} %copy-done.38) | copy-start | bytes 1540
  (33 other events, 254.1 us)
Sparse Core Ops, SparseCore 0:
  30.4 36.3 all-gather.18
  68.7 22.7 all-gather.26
  93.4 23.9 all-gather.28
  121.0 35.4 reduce-scatter.11
  158.2 31.0 all-gather.32
  191.3 37.0 all-gather.20
  230.2 31.0 all-gather.30
  262.9 37.0 all-gather.22
  301.8 31.0 all-gather.34
  345.9 35.4 reduce-scatter.15
  385.7 35.8 all-gather.24
  424.9 44.8 reduce-scatter.31
  473.2 46.0 reduce-scatter.29
  522.6 46.0 reduce-scatter.27
  571.6 34.9 reduce-scatter.23
  610.2 34.9 reduce-scatter.21
  648.2 36.6 reduce-scatter.25
  688.0 36.6 reduce-scatter.19
  727.0 35.4 reduce-scatter.17
  764.6 34.4 reduce-scatter.13
where the time goes:
time: 810 us; the launch traced here: 809 us
  waiting for transfers between devices  605 us (75%)
  matrix products  75 us (9%)
  blocking collectives  65.6 us (8%)
  other arithmetic  32.9 us (4%)
  between operations  16.2 us (2%)
  local copies, waits for them, and re-layouts  12.8 us (2%)
    reduce_scatter x4, waiting for transfers between devices, settle(): lax.psum_scatter(terms_in.astype(jnp.bfloat16), 'dp', scatter_dimension=0...  111 us
    all_gather x4, waiting for transfers between devices, spread(): return lax.all_gather(rows_in, 'dp', axis=0, tiled=True)  105 us
    reduce_scatter x1, waiting for transfers between devices, body(): lax.psum_scatter(terms[7].astype(jnp.bfloat16), 'fsdp', scatter_dimension...  47.6 us
    reduce_scatter x1, waiting for transfers between devices, body(): lax.psum_scatter(terms[6].astype(jnp.bfloat16), 'fsdp', scatter_dimension...  47.3 us
    reduce_scatter x1, waiting for transfers between devices, body(): lax.psum_scatter(terms[4].astype(jnp.bfloat16), 'fsdp', scatter_dimension...  38.2 us
    reduce_scatter x1, waiting for transfers between devices, body(): lax.psum_scatter(terms[1].astype(jnp.bfloat16), 'fsdp', scatter_dimension...  38.2 us
    reduce_scatter x1, waiting for transfers between devices, body(): lax.psum_scatter(terms[2].astype(jnp.bfloat16), 'fsdp', scatter_dimension...  37 us
    reduce_scatter x1, waiting for transfers between devices, body(): lax.psum_scatter(terms[3].astype(jnp.bfloat16), 'fsdp', scatter_dimension...  36 us
  transfers between devices with their start and end apart: 20, of which 20 were waited for; matrix products, arithmetic and copies ran while one was open for 11% of the time, Pallas kernels for 0%

commit v1 on v0

--- a/solution.py
+++ b/solution.py
@@ -9,6 +9,19 @@
 EPSILON = 1e-05
 ROPE_BASE = 100000.0
 NEG_FILL = -1e30
+
+
+def collect(array, axis, dim):
+    ways = lax.axis_size(axis)
+    up = [(d, (d + 1) % ways) for d in range(ways)]
+    down = [(d, (d - 1) % ways) for d in range(ways)]
+    earlier, later = ([array], [array])
+    for _ in range(ways // 2):
+        earlier.append(lax.ppermute(earlier[-1], axis, up))
+    for _ in range((ways - 1) // 2):
+        later.append(lax.ppermute(later[-1], axis, down))
+    line = jnp.concatenate([*earlier[::-1], *later[1:]], axis=dim)
+    return jnp.roll(line, (lax.axis_index(axis) - ways // 2) * array.shape[dim], axis=dim)
 
 
 def layout(seq_lengths, rows_here):
@@ -322,7 +335,7 @@
     shards = (attn_gain, w_query, w_key, w_value, w_out, mlp_gain, w_gate, w_up, w_down)
 
     def spread(rows_in):
-        return lax.all_gather(rows_in, "dp", axis=0, tiled=True)
+        return collect(rows_in, "dp", 0)
 
     def settle(terms_in):
         return lax.psum_scatter(

time: 810 us -> 670 us (0.83); the launches traced: 809 us -> 660 us
  waiting for transfers between devices: 605 us -> 408 us
  other arithmetic: 32.9 us -> 59.1 us
  starting transfers between devices: 1.47 us -> 22.3 us
    all_gather x4 -> x0, waiting for transfers between devices: 105 us -> none  [spread(): return lax.all_gather(rows_in, 'dp', axis=0, tiled=True)]
    ppermute x0 -> x12, waiting for transfers between devices: none -> 63.6 us  [the longest x8 49 us: collect(): earlier.append(lax.ppermute(earlier[-1], axis, up))]
    reduce_scatter x1, waiting for transfers between devices: 47.6 us -> 18.9 us  [body(): lax.psum_scatter(terms[7].astype(jnp.bfloat16), 'fsdp', scatter_dimension...]
    all_gather x1, waiting for transfers between devices: 27.4 us -> 0.01 us  [fetch_fsdp(): lax.all_gather(shards[6][layer_idx], 'fsdp', axis=0, tiled=True)]
    all_gather x1, waiting for transfers between devices: 27.2 us -> 0.01 us  [fetch_fsdp(): lax.all_gather(shards[7][layer_idx], 'fsdp', axis=0, tiled=True)]
    concatenate x0 -> x3, other arithmetic: none -> 25.5 us  [collect(): jnp.roll(line, (lax.axis_index(axis) - ways // 2) * array.shape[dim], axi...]
    ppermute x0 -> x12, starting transfers between devices: none -> 21.2 us  [the longest x4 14.4 us: collect(): later.append(lax.ppermute(later[-1], axis, down))]
    all_gather x1, waiting for transfers between devices: 20.8 us -> 0.01 us  [fetch_fsdp(): lax.all_gather(shards[4][layer_idx], 'fsdp', axis=1, tiled=True)]
  transfers between devices with their start and end apart: 20 -> 28, of which waited for: 20 -> 20; matrix products, arithmetic and copies ran while one was open for 11% -> 19% of each run, Pallas kernels for 0% -> 0%
where the time goes in v1:
time: 670 us; the launch traced here: 660 us
  waiting for transfers between devices  408 us (61%)
  matrix products  73.6 us (11%)
  blocking collectives  67.4 us (10%)
  other arithmetic  59.1 us (9%)
  starting transfers between devices  22.3 us (3%)
  between operations  16.3 us (2%)
  local copies, waits for them, and re-layouts  13.2 us (2%)
    reduce_scatter x4, waiting for transfers between devices, settle(): lax.psum_scatter(terms_in.astype(jnp.bfloat16), 'dp', scatter_dimension=0...  99 us
    ppermute x8, waiting for transfers between devices, collect(): earlier.append(lax.ppermute(earlier[-1], axis, up))  49 us
    reduce_scatter x1, waiting for transfers between devices, body(): lax.psum_scatter(terms[6].astype(jnp.bfloat16), 'fsdp', scatter_dimension...  47.4 us
    reduce_scatter x1, waiting for transfers between devices, body(): lax.psum_scatter(terms[4].astype(jnp.bfloat16), 'fsdp', scatter_dimension...  38.4 us
    reduce_scatter x1, waiting for transfers between devices, body(): lax.psum_scatter(terms[1].astype(jnp.bfloat16), 'fsdp', scatter_dimension...  38.2 us
    reduce_scatter x1, waiting for transfers between devices, body(): lax.psum_scatter(terms[2].astype(jnp.bfloat16), 'fsdp', scatter_dimension...  37 us
    reduce_scatter x1, waiting for transfers between devices, body(): lax.psum_scatter(terms[3].astype(jnp.bfloat16), 'fsdp', scatter_dimension...  36.2 us
    unnamed x2, blocking collectives  27.9 us
  transfers between devices with their start and end apart: 28, of which 20 were waited for; matrix products, arithmetic and copies ran while one was open for 19% of the time, Pallas kernels for 0%

profile of v1, /device:TPU:0, one launch (start us, length us, event | category | flops | bytes accessed | tf_op | source)
XLA Modules:
  0.0 660.1 jit_solution(5735759648533153283)
XLA Ops:
  11.8 15.4 %all-reduce.6 = (bf16[1536]{0:T(1024)(128)(2,1)S(1)}, bf16[1536]{0:T(1024)(128)(2,1)S(1)}) all-reduce(bf16[1536]{0:T(1024)(128)(2,1)S(1)} %dynamic-update-slice, bf16[1536]{0:T(1024)(128)(2,1)S(1)} %dynamic-update-slice.1), channel_id=2, replica_groups=mesh['fsdp'=8,'dp'=4] {'fsdp'}, use_global_device_ids=true, to_apply=%add | all-reduce | flops 3072 | bytes 12288
  35.1 9.8 %all-gather.2 = bf16[1,1536,192]{2,1,0:T(8,128)(2,1)S(1)} all-gather(bf16[1,192,192]{2,1,0:T(8,128)(2,1)} %param.19), channel_id=4, replica_groups=mesh['fsdp'=8,'dp'=4] {'fsdp'}, dimensions={1}, use_global_device_ids=true | all-gather | bytes 663552 | tf_op jit(solution)/shard_map/all_gather | solution.py:282
  51.0 12.5 %all-gather.1 = bf16[1,1536,192]{2,1,0:T(8,128)(2,1)S(1)} all-gather(bf16[1,192,192]{2,1,0:T(8,128)(2,1)} %param.20), channel_id=3, replica_groups=mesh['fsdp'=8,'dp'=4] {'fsdp'}, dimensions={1}, use_global_device_ids=true | all-gather | bytes 663552 | tf_op jit(solution)/shard_map/all_gather | solution.py:283
  64.5 6.5 fusion.42
  85.2 39.5 %reduce-scatter.12.cloned.1.call-done = bf16[128,1536]{1,0:T(8,128)(2,1)} async-done(((bf16[512,1536]{1,0:T(8,128)(2,1)}), bf16[128,1536]{1,0:T(8,128)(2,1)}) %reduce-scatter.12.cloned.1.call-update) | async-done | bytes 393232 | tf_op jit(solution)/shard_map/reduce_scatter | solution.py:341
  134.7 6.2 collective-permute-done.3
  141.1 7.4 %collective-permute-done.8 = bf16[128,1536]{1,0:T(8,128)(2,1)S(1)} collective-permute-done((bf16[128,1536]{1,0:T(8,128)(2,1)S(1)}, bf16[128,1536]{1,0:T(8,128)(2,1)S(1)}, u32[]{:S(2)}, u32[]{:S(2)}) %collective-permute-start.8) | collective-permute-done | bytes 393248 | tf_op jit(solution)/shard_map/ppermute | solution.py:22
  148.5 9.3 %collective-permute-done.7 = bf16[128,1536]{1,0:T(8,128)(2,1)S(1)} collective-permute-done((bf16[128,1536]{1,0:T(8,128)(2,1)}, bf16[128,1536]{1,0:T(8,128)(2,1)S(1)}, u32[]{:S(2)}, u32[]{:S(2)}) %collective-permute-start.7) | collective-permute-done | bytes 393248 | tf_op jit(solution)/shard_map/ppermute | solution.py:20
  157.8 6.0 collective-permute-done.5
  163.8 10.0 %collective-permute-done.4 = bf16[128,1536]{1,0:T(8,128)(2,1)S(1)} collective-permute-done((bf16[128,1536]{1,0:T(8,128)(2,1)S(1)}, bf16[128,1536]{1,0:T(8,128)(2,1)S(1)}, u32[]{:S(2)}, u32[]{:S(2)}) %collective-permute-start.4) | collective-permute-done | bytes 393248 | tf_op jit(solution)/shard_map/ppermute | solution.py:20
  173.8 12.0 %fusion.28 = (bf16[512,1536]{1,0:T(8,128)(2,1)}, bf16[512,1536]{1,0:T(8,128)(2,1)}) fusion(s32[]{:T(128)S(6)} %select_n.33, bf16[128,1536]{1,0:T(8,128)(2,1)S(1)} %collective-permute-done.7, bf16[128,1536]{1,0:T(8,128)(2,1)} %collective-permute-done.6, bf16[128,1536]{1,0:T(8,128)(2,1)S(1)} %copy-done.6, bf16[128,1536]{1,0:T(8,128)(2,1)S(1)} %collective-permute-done.8, ...), kind=kLoop, calls=%fused_computation.71 | loop fusion | flops 25165824 | bytes 6291460 | tf_op jit(solution)/shard_map/jit(_roll_dynamic)/concatenate | solution.py:24
  185.8 5.6 fusion.5
  191.3 5.5 fusion.9
  196.9 27.1 %all-gather.23.cloned.1.call-done = bf16[1,1024,1536]{1,2,0:T(8,128)(2,1)} async-done(((bf16[1,1024,192]{1,2,0:T(8,128)(2,1)}), bf16[1,1024,1536]{1,2,0:T(8,128)(2,1)}) %all-gather.23.cloned.1.call-update) | async-done | bytes 3145744 | tf_op jit(solution)/shard_map/all_gather | solution.py:287
  224.0 7.2 %multiply_convert_fusion = (bf16[512,1024]{1,0:T(8,128)(2,1)S(1)}, bf16[512,1024]{1,0:T(8,128)(2,1)S(1)}, bf16[512,1024]{1,0:T(8,128)(2,1)}) fusion(f32[512,1024]{1,0:T(8,128)} %fusion.9, f32[512,1024]{1,0:T(8,128)} %fusion.5, bf16[512,1536]{1,0:T(8,128)(2,1)} %get-tuple-element.42, bf16[1,1024,1536]{1,2,0:T(8,128)(2,1)} %all-gather.23.cloned.1.call-done), kind=kOutput, calls=%fused_computation.57 | convolution fusion | flops 1619001344 | bytes 12058624 | tf_op jit(solution)/shard_map/dot_general | solution.py:72
  237.2 5.3 convolution_convert_fusion
  242.6 5.4 convolution_convert_fusion.1
  248.1 5.2 convolution_convert_fusion.2
  253.3 19.2 %reduce-scatter.16.cloned.1.call-done = bf16[128,1536]{1,0:T(8,128)(2,1)} async-done(((bf16[512,1536]{1,0:T(8,128)(2,1)}), bf16[128,1536]{1,0:T(8,128)(2,1)}) %reduce-scatter.16.cloned.1.call-update) | async-done | bytes 393232 | tf_op jit(solution)/shard_map/reduce_scatter | solution.py:341
  279.4 10.0 %collective-permute-done.9 = bf16[128,1536]{1,0:T(8,128)(2,1)S(1)} collective-permute-done((bf16[128,1536]{1,0:T(8,128)(2,1)S(1)}, bf16[128,1536]{1,0:T(8,128)(2,1)S(1)}, u32[]{:S(2)}, u32[]{:S(2)}) %collective-permute-start.9) | collective-permute-done | bytes 393248 | tf_op jit(solution)/shard_map/ppermute | solution.py:20
  294.6 10.1 %collective-permute-done.10 = bf16[128,1536]{1,0:T(8,128)(2,1)S(1)} collective-permute-done((bf16[128,1536]{1,0:T(8,128)(2,1)S(1)}, bf16[128,1536]{1,0:T(8,128)(2,1)S(1)}, u32[]{:S(2)}, u32[]{:S(2)}) %collective-permute-start.10) | collective-permute-done | bytes 393248 | tf_op jit(solution)/shard_map/ppermute | solution.py:20
  304.7 7.0 %fusion.21 = bf16[512,1536]{1,0:T(8,128)(2,1)S(1)} fusion(s32[]{:T(128)S(6)} %select_n.33, bf16[128,1536]{1,0:T(8,128)(2,1)S(1)} %collective-permute-done.10, bf16[128,1536]{1,0:T(8,128)(2,1)S(1)} %collective-permute-done.9, bf16[128,1536]{1,0:T(8,128)(2,1)S(1)} %fusion.103, bf16[128,1536]{1,0:T(8,128)(2,1)S(1)} %collective-permute-done.11), kind=kLoop, calls=%fused_computation.64 | loop fusion | flops 12582912 | bytes 3145732 | tf_op jit(solution)/shard_map/jit(_roll_dynamic)/concatenate | solution.py:24
  343.5 5.2 fusion.11
  351.4 18.9 %reduce-scatter.30.cloned.1.call-done = bf16[192,1024]{1,0:T(8,128)(2,1)} async-done(((bf16[1536,1024]{1,0:T(8,128)(2,1)}), bf16[192,1024]{1,0:T(8,128)(2,1)}) %reduce-scatter.30.cloned.1.call-update) | async-done | bytes 393232 | tf_op jit(solution)/shard_map/reduce_scatter | solution.py:381
  372.3 47.4 %reduce-scatter.28.cloned.1.call-done = bf16[192,1024]{1,0:T(8,128)(2,1)} async-done(((bf16[1536,1024]{1,0:T(8,128)(2,1)}), bf16[192,1024]{1,0:T(8,128)(2,1)}) %reduce-scatter.28.cloned.1.call-update) | async-done | bytes 393232 | tf_op jit(solution)/shard_map/reduce_scatter | solution.py:378
  421.6 36.2 %reduce-scatter.24.cloned.1.call-done = bf16[192,192]{1,0:T(8,128)(2,1)} async-done(((bf16[1536,192]{1,0:T(8,128)(2,1)}), bf16[192,192]{1,0:T(8,128)(2,1)}) %reduce-scatter.24.cloned.1.call-update) | async-done | bytes 73744 | tf_op jit(solution)/shard_map/reduce_scatter | solution.py:372
  459.4 37.0 %reduce-scatter.22.cloned.1.call-done = bf16[192,192]{1,0:T(8,128)(2,1)} async-done(((bf16[1536,192]{1,0:T(8,128)(2,1)}), bf16[192,192]{1,0:T(8,128)(2,1)}) %reduce-scatter.22.cloned.1.call-update) | async-done | bytes 73744 | tf_op jit(solution)/shard_map/reduce_scatter | solution.py:369
  497.9 38.4 %reduce-scatter.26.cloned.1.call-done = bf16[384,192]{0,1:T(8,128)(2,1)} async-done(((bf16[384,1536]{0,1:T(8,128)(2,1)}), bf16[384,192]{0,1:T(8,128)(2,1)}) %reduce-scatter.26.cloned.1.call-update) | async-done | bytes 147472 | tf_op jit(solution)/shard_map/reduce_scatter | solution.py:375
  537.9 38.2 %reduce-scatter.20.cloned.1.call-done = bf16[192,384]{1,0:T(8,128)(2,1)} async-done(((bf16[1536,384]{1,0:T(8,128)(2,1)}), bf16[192,384]{1,0:T(8,128)(2,1)}) %reduce-scatter.20.cloned.1.call-update) | async-done | bytes 147472 | tf_op jit(solution)/shard_map/reduce_scatter | solution.py:366
  577.7 36.0 %reduce-scatter.18.cloned.1.call-done = bf16[128,1536]{1,0:T(8,128)(2,1)} async-done(((bf16[512,1536]{1,0:T(8,128)(2,1)}), bf16[128,1536]{1,0:T(8,128)(2,1)}) %reduce-scatter.18.cloned.1.call-update) | async-done | bytes 393232 | tf_op jit(solution)/shard_map/reduce_scatter | solution.py:341
  615.1 17.3 %all-reduce.4 = (bf16[1536]{0:T(1024)(128)(2,1)S(1)}, bf16[1536]{0:T(1024)(128)(2,1)S(1)}) all-reduce(f32[1536]{0:T(1024)S(1)} %get-tuple-element.14, f32[1536]{0:T(1024)S(1)} %get-tuple-element.12), channel_id=1, replica_groups=mesh['fsdp'=8,'dp'=4] {'dp'}, use_global_device_ids=true, to_apply=%region_15.17 | all-reduce | flops 3072 | bytes 18432 | tf_op jit(solution)/shard_map/psum | solution.py:364
  632.4 12.4 %all-reduce.5 = (bf16[1536]{0:T(1024)(128)(2,1)S(1)}, bf16[1536]{0:T(1024)(128)(2,1)S(1)}) all-reduce(bf16[1536]{0:T(1024)(128)(2,1)S(1)} %get-tuple-element.16, bf16[1536]{0:T(1024)(128)(2,1)S(1)} %get-tuple-element.17), channel_id=15, replica_groups=mesh['fsdp'=8,'dp'=4] {'fsdp'}, use_global_device_ids=true, to_apply=%region_16.18.clone | all-reduce | flops 3072 | bytes 12288
  (191 shorter events, 114.8 us)
Async XLA Ops:
  7.2 66.1 %all-gather.15.cloned.1.call-start = ((), (), s32[]{:S(2)}) async-start(), calls=%async_computation.22 | async-start | bytes 1327104 | tf_op jit(solution)/shard_map/all_gather | solution.py:281
  7.9 71.7 %all-gather.17.cloned.1.call-start = ((), (), s32[]{:S(2)}) async-start(), calls=%async_computation.23 | async-start | bytes 1327104 | tf_op jit(solution)/shard_map/all_gather | solution.py:284
  29.6 34.9 %collective-permute-start.2 = (bf16[128,1536]{1,0:T(8,128)(2,1)S(1)}, bf16[128,1536]{1,0:T(8,128)(2,1)S(1)}, u32[]{:S(2)}, u32[]{:S(2)}) collective-permute-start(bf16[128,1536]{1,0:T(8,128)(2,1)S(1)} %fusion.75), channel_id=1, source_target_pairs={{0,3},{1,0},{2,1},{3,2},{4,7},{5,4},{6,5},{7,6},{8,11},{9,8},{10,9... | collective-permute-start | bytes 1179656 | tf_op jit(solution)/shard_map/ppermute | solution.py:22
  33.3 15.9 %collective-permute-start = (bf16[128,1536]{1,0:T(8,128)(2,1)S(1)}, bf16[128,1536]{1,0:T(8,128)(2,1)S(1)}, u32[]{:S(2)}, u32[]{:S(2)}) collective-permute-start(bf16[128,1536]{1,0:T(8,128)(2,1)S(1)} %fusion.75), channel_id=1, source_target_pairs={{0,1},{1,2},{2,3},{3,0},{4,5},{5,6},{6,7},{7,4},{8,9},{9,10},{10,1... | collective-permute-start | bytes 1179656 | tf_op jit(solution)/shard_map/ppermute | solution.py:20
  33.3 91.4 %reduce-scatter.12.cloned.1.call-start = ((), (), s32[]{:S(2)}) async-start(), calls=%async_computation.11 | async-start | bytes 1966080 | tf_op jit(solution)/shard_map/reduce_scatter | solution.py:341
  49.2 15.4 %collective-permute-start.1 = (bf16[128,1536]{1,0:T(8,128)(2,1)S(1)}, bf16[128,1536]{1,0:T(8,128)(2,1)}, u32[]{:S(2)}, u32[]{:S(2)}) collective-permute-start(bf16[128,1536]{1,0:T(8,128)(2,1)S(1)} %collective-permute-done), channel_id=1, source_target_pairs={{0,1},{1,2},{2,3},{3,0},{4,5},{5,6},{6,7},{7,4},{8,9},{9,10},{10,1... | collective-permute-start | bytes 1179656 | tf_op jit(solution)/shard_map/ppermute | solution.py:20
  79.6 45.1 %copy-start = (bf16[128,1536]{1,0:T(8,128)(2,1)S(1)}, bf16[128,1536]{1,0:T(8,128)(2,1)}, u32[]{:S(2)}) copy-start(bf16[128,1536]{1,0:T(8,128)(2,1)} %param.14) | copy-start | bytes 1179652
  83.3 102.5 %all-gather.21.cloned.1.call-start = ((), (), s32[]{:S(2)}) async-start(), calls=%async_computation.25 | async-start | bytes 3538944 | tf_op jit(solution)/shard_map/all_gather | solution.py:286
  83.9 107.5 %all-gather.19.cloned.1.call-start = ((), (), s32[]{:S(2)}) async-start(), calls=%async_computation.24 | async-start | bytes 3538944 | tf_op jit(solution)/shard_map/all_gather | solution.py:285
  84.4 139.6 %all-gather.23.cloned.1.call-start = ((), (), s32[]{:S(2)}) async-start(), calls=%async_computation.26 | async-start | bytes 3538944 | tf_op jit(solution)/shard_map/all_gather | solution.py:287
  85.0 187.5 %reduce-scatter.16.cloned.1.call-start = ((), (), s32[]{:S(2)}) async-start(), calls=%async_computation.13 | async-start | bytes 1966080 | tf_op jit(solution)/shard_map/reduce_scatter | solution.py:341
  85.1 45.8 %collective-permute-start.6 = (bf16[128,1536]{1,0:T(8,128)(2,1)S(1)}, bf16[128,1536]{1,0:T(8,128)(2,1)}, u32[]{:S(2)}, u32[]{:S(2)}) collective-permute-start(bf16[128,1536]{1,0:T(8,128)(2,1)S(1)} %copy-done.6), channel_id=1, source_target_pairs={{0,1},{1,2},{2,3},{3,0},{4,5},{5,6},{6,7},{7,4},{8,9},{9,10},{10,1... | collective-permute-start | bytes 1179656 | tf_op jit(solution)/shard_map/ppermute | solution.py:20
  127.0 13.9 %collective-permute-start.3 = (bf16[128,1536]{1,0:T(8,128)(2,1)S(1)}, bf16[128,1536]{1,0:T(8,128)(2,1)S(1)}, u32[]{:S(2)}, u32[]{:S(2)}) collective-permute-start(bf16[128,1536]{1,0:T(8,128)(2,1)S(1)} %multiply_convert_fusion.3), channel_id=1, source_target_pairs={{0,1},{1,2},{2,3},{3,0},{4,5},{5,6},{6,7},{7,4},{8,9},{9,10},{10,1... | collective-permute-start | bytes 1179656 | tf_op jit(solution)/shard_map/ppermute | solution.py:20
  127.6 20.9 %collective-permute-start.8 = (bf16[128,1536]{1,0:T(8,128)(2,1)S(1)}, bf16[128,1536]{1,0:T(8,128)(2,1)S(1)}, u32[]{:S(2)}, u32[]{:S(2)}) collective-permute-start(bf16[128,1536]{1,0:T(8,128)(2,1)S(1)} %copy-done.6), channel_id=1, source_target_pairs={{0,3},{1,0},{2,1},{3,2},{4,7},{5,4},{6,5},{7,6},{8,11},{9,8},{10,9... | collective-permute-start | bytes 1179656 | tf_op jit(solution)/shard_map/ppermute | solution.py:22
  130.9 26.9 %collective-permute-start.7 = (bf16[128,1536]{1,0:T(8,128)(2,1)}, bf16[128,1536]{1,0:T(8,128)(2,1)S(1)}, u32[]{:S(2)}, u32[]{:S(2)}) collective-permute-start(bf16[128,1536]{1,0:T(8,128)(2,1)} %collective-permute-done.6), channel_id=1, source_target_pairs={{0,1},{1,2},{2,3},{3,0},{4,5},{5,6},{6,7},{7,4},{8,9},{9,10},{10,1... | collective-permute-start | bytes 1179656 | tf_op jit(solution)/shard_map/ppermute | solution.py:20
  130.9 32.9 %collective-permute-start.5 = (bf16[128,1536]{1,0:T(8,128)(2,1)S(1)}, bf16[128,1536]{1,0:T(8,128)(2,1)S(1)}, u32[]{:S(2)}, u32[]{:S(2)}) collective-permute-start(bf16[128,1536]{1,0:T(8,128)(2,1)S(1)} %multiply_convert_fusion.3), channel_id=1, source_target_pairs={{0,3},{1,0},{2,1},{3,2},{4,7},{5,4},{6,5},{7,6},{8,11},{9,8},{10,9... | collective-permute-start | bytes 1179656 | tf_op jit(solution)/shard_map/ppermute | solution.py:22
  140.9 32.9 %collective-permute-start.4 = (bf16[128,1536]{1,0:T(8,128)(2,1)S(1)}, bf16[128,1536]{1,0:T(8,128)(2,1)S(1)}, u32[]{:S(2)}, u32[]{:S(2)}) collective-permute-start(bf16[128,1536]{1,0:T(8,128)(2,1)S(1)} %collective-permute-done.3), channel_id=1, source_target_pairs={{0,1},{1,2},{2,3},{3,0},{4,5},{5,6},{6,7},{7,4},{8,9},{9,10},{10,1... | collective-permute-start | bytes 1179656 | tf_op jit(solution)/shard_map/ppermute | solution.py:20
  236.9 112.5 %reduce-scatter.32.cloned.1.call-start = ((), (), s32[]{:S(2)}) async-start(), calls=%async_computation.21 | async-start | bytes 3538944 | tf_op jit(solution)/shard_map/reduce_scatter | solution.py:384
  242.6 127.8 %reduce-scatter.30.cloned.1.call-start = ((), (), s32[]{:S(2)}) async-start(), calls=%async_computation.20 | async-start | bytes 3538944 | tf_op jit(solution)/shard_map/reduce_scatter | solution.py:381
  248.0 171.6 %reduce-scatter.28.cloned.1.call-start = ((), (), s32[]{:S(2)}) async-start(), calls=%async_computation.19 | async-start | bytes 3538944 | tf_op jit(solution)/shard_map/reduce_scatter | solution.py:378
  253.3 204.5 %reduce-scatter.24.cloned.1.call-start = ((), (), s32[]{:S(2)}) async-start(), calls=%async_computation.17 | async-start | bytes 884736 | tf_op jit(solution)/shard_map/reduce_scatter | solution.py:372
  272.5 40.4 %copy-start.13 = (bf16[1,384,1536]{1,2,0:T(8,128)(2,1)S(1)}, bf16[1,384,1536]{1,2,0:T(8,128)(2,1)}, u32[]{:S(2)}) copy-start(bf16[1,384,1536]{1,2,0:T(8,128)(2,1)} %all-gather.17.cloned.1.call-done) | copy-start | bytes 3538948
  275.5 13.8 %collective-permute-start.9 = (bf16[128,1536]{1,0:T(8,128)(2,1)S(1)}, bf16[128,1536]{1,0:T(8,128)(2,1)S(1)}, u32[]{:S(2)}, u32[]{:S(2)}) collective-permute-start(bf16[128,1536]{1,0:T(8,128)(2,1)S(1)} %fusion.103), channel_id=1, source_target_pairs={{0,1},{1,2},{2,3},{3,0},{4,5},{5,6},{6,7},{7,4},{8,9},{9,10},{10,1... | collective-permute-start | bytes 1179656 | tf_op jit(solution)/shard_map/ppermute | solution.py:20
  275.7 18.9 %collective-permute-start.11 = (bf16[128,1536]{1,0:T(8,128)(2,1)S(1)}, bf16[128,1536]{1,0:T(8,128)(2,1)S(1)}, u32[]{:S(2)}, u32[]{:S(2)}) collective-permute-start(bf16[128,1536]{1,0:T(8,128)(2,1)S(1)} %fusion.103), channel_id=1, source_target_pairs={{0,3},{1,0},{2,1},{3,2},{4,7},{5,4},{6,5},{7,6},{8,11},{9,8},{10,9... | collective-permute-start | bytes 1179656 | tf_op jit(solution)/shard_map/ppermute | solution.py:22
  289.3 15.4 %collective-permute-start.10 = (bf16[128,1536]{1,0:T(8,128)(2,1)S(1)}, bf16[128,1536]{1,0:T(8,128)(2,1)S(1)}, u32[]{:S(2)}, u32[]{:S(2)}) collective-permute-start(bf16[128,1536]{1,0:T(8,128)(2,1)S(1)} %collective-permute-done.9), channel_id=1, source_target_pairs={{0,1},{1,2},{2,3},{3,0},{4,5},{5,6},{6,7},{7,4},{8,9},{9,10},{10,1... | collective-permute-start | bytes 1179656 | tf_op jit(solution)/shard_map/ppermute | solution.py:20
  325.4 171.0 %reduce-scatter.22.cloned.1.call-start = ((), (), s32[]{:S(2)}) async-start(), calls=%async_computation.16 | async-start | bytes 884736 | tf_op jit(solution)/shard_map/reduce_scatter | solution.py:369
  328.4 207.9 %reduce-scatter.26.cloned.1.call-start = ((), (), s32[]{:S(2)}) async-start(), calls=%async_computation.18 | async-start | bytes 1327104 | tf_op jit(solution)/shard_map/reduce_scatter | solution.py:375
  332.4 243.7 %reduce-scatter.20.cloned.1.call-start = ((), (), s32[]{:S(2)}) async-start(), calls=%async_computation.15 | async-start | bytes 1327104 | tf_op jit(solution)/shard_map/reduce_scatter | solution.py:366
  337.8 275.9 %reduce-scatter.18.cloned.1.call-start = ((), (), s32[]{:S(2)}) async-start(), calls=%async_computation.14 | async-start | bytes 1966080 | tf_op jit(solution)/shard_map/reduce_scatter | solution.py:341
  343.4 307.0 %reduce-scatter.14.cloned.1.call-start = ((), (), s32[]{:S(2)}) async-start(), calls=%async_computation.12 | async-start | bytes 1966080 | tf_op jit(solution)/shard_map/reduce_scatter | solution.py:341
  348.7 301.7 %copy-start.7 = (bf16[128,1536]{1,0:T(8,128)(2,1)S(1)}, bf16[128,1536]{1,0:T(8,128)(2,1)}, u32[]{:S(2)}) copy-start(bf16[128,1536]{1,0:T(8,128)(2,1)} %param.16) | copy-start | bytes 1179652
  348.7 301.7 %copy-start.8 = (bf16[128,1536]{1,0:T(8,128)(2,1)S(1)}, bf16[128,1536]{1,0:T(8,128)(2,1)}, u32[]{:S(2)}) copy-start(bf16[128,1536]{1,0:T(8,128)(2,1)} %reduce-scatter.16.cloned.1.call-done) | copy-start | bytes 1179652
  (23 other events, 122.5 us)
Sparse Core Ops, SparseCore 0:
  9.9 26.7 all-gather.14
  38.5 25.6 all-gather.16
  83.4 41.2 reduce-scatter.11
  126.4 29.6 all-gather.20
  157.9 32.1 all-gather.18
  191.8 32.1 all-gather.22
  237.1 35.4 reduce-scatter.15
  275.9 44.9 reduce-scatter.31
  324.2 46.0 reduce-scatter.29
  373.6 46.0 reduce-scatter.27
  422.8 34.9 reduce-scatter.23
  461.4 34.9 reduce-scatter.21
  499.6 36.6 reduce-scatter.25
  539.4 36.6 reduce-scatter.19
  578.2 35.4 reduce-scatter.17
  615.9 34.4 reduce-scatter.13
